TPU v7x, 32 devices: a whole 2x2x4 slice. The times are simulated.
32 devices in a mesh: ka: 16 (over z, x, core), sp: 2 (over y).
Axes of the slice: x: 2, y: 2, z: 4, core: 2. Of those that a mesh axis runs over, the one named last changes fastest.
Arguments:
- bloch_index: int32 [16, 2], P('ka'), may hold values from 0 to 63
- material: int32 [32, 64, 128], P('sp'), may hold values from 0 to 2
- permittivity: float32 [3], replicated, may hold values from 1 to 12
- absorption_peak: float32 [1], replicated, may hold values from 0.25 to 2
- source_sheet: float32 [16, 2, 32, 64], P('ka', None, 'sp'), may hold values from -6 to 6
- waveform: float32 [10], replicated, may hold values from -6 to 6
- electric_in: bfloat16 [16, 6, 32, 64, 128], P('ka', None, 'sp'), may hold values from -12 to 12
- magnetic_in: bfloat16 [16, 6, 32, 64, 128], P('ka', None, 'sp'), may hold values from -12 to 12
Outputs:
- electric_out: float32 [16, 6, 32, 64, 128], P('ka', None, 'sp')
- magnetic_out: float32 [16, 6, 32, 64, 128], P('ka', None, 'sp')
- reflected: float32 [16, 2], P('ka')
- reflected_mean: float32 [2], replicated
All inputs are finite; a program needn't handle non-finite values.
Results may differ from a plain program's by a relative error of at most 0.0003.
Values sent between devices are 32-bit elements; how exact they have to be, the bound alone decides.
A program may use at most 64 MiB of HBM per device.

v0:
```python
import jax
import jax.numpy as jnp
from jax import lax
from jax.sharding import PartitionSpec as P

PML = 16
INTERVAL = 5
NSNAP = 2
MPHASE = 64
NMAT = 3


TIME_STEP = 0.5


def shifted_2(value, axis, steps):
    count = lax.axis_size(axis)
    pairs = [(source, (source + steps) % count) for source in range(count)]
    return lax.ppermute(value, axis, pairs)


def rotate(couple, cosine, sine):
    return (couple[0] * cosine - couple[1] * sine, couple[0] * sine + couple[1] * cosine)


def subtract(left, right):
    return (left[0] - right[0], left[1] - right[1])


def position(values, along):
    return lax.broadcasted_iota(jnp.int32, values.shape, along)


def roll_couple(couple, amount, along):
    return tuple((jnp.roll(values, amount, axis=along) for values in couple))


def above_cell(couple, beyond, along):
    length = couple[0].shape[along]
    rolled = roll_couple(couple, -1, along)
    last = position(couple[0], along) == length - 1
    return tuple((jnp.where(last, edge, moved) for edge, moved in zip(beyond, rolled)))


def below_cell(couple, beyond, along):
    rolled = roll_couple(couple, 1, along)
    first = position(couple[0], along) == 0
    return tuple((jnp.where(first, edge, moved) for edge, moved in zip(beyond, rolled)))


def forward_wrap(couple, along, cosine, sine):
    length = couple[0].shape[along]
    rolled = roll_couple(couple, -1, along)
    turned = rotate(rolled, cosine, sine)
    last = position(couple[0], along) == length - 1
    shifted = tuple((jnp.where(last, edge, moved) for edge, moved in zip(turned, rolled)))
    return subtract(shifted, couple)


def backward_wrap(couple, along, cosine, sine):
    rolled = roll_couple(couple, 1, along)
    turned = rotate(rolled, cosine, -sine)
    first = position(couple[0], along) == 0
    shifted = tuple((jnp.where(first, edge, moved) for edge, moved in zip(turned, rolled)))
    return subtract(couple, shifted)


def forward_open(couple):
    along = couple[0].ndim - 1
    length = couple[0].shape[along]
    rolled = roll_couple(couple, -1, along)
    last = position(couple[0], along) == length - 1
    shifted = tuple((jnp.where(last, 0.0, moved) for moved in rolled))
    return subtract(shifted, couple)


def backward_open(couple):
    along = couple[0].ndim - 1
    rolled = roll_couple(couple, 1, along)
    first = position(couple[0], along) == 0
    shifted = tuple((jnp.where(first, 0.0, moved) for moved in rolled))
    return subtract(couple, shifted)


def electric_curl(electric, beyond_y, beyond_z, cosine, sine):
    ex_part, ey_part, ez_part = electric
    across = ex_part[0].ndim - 3
    sideways = across + 1
    dx_ey = subtract(above_cell(ey_part, beyond_y, across), ey_part)
    dx_ez = subtract(above_cell(ez_part, beyond_z, across), ez_part)
    return (
        subtract(forward_wrap(ez_part, sideways, cosine, sine), forward_open(ey_part)),
        subtract(forward_open(ex_part), dx_ez),
        subtract(dx_ey, forward_wrap(ex_part, sideways, cosine, sine)),
    )


def magnetic_curl(magnetic, behind_y, behind_z, cosine, sine):
    hx_part, hy_part, hz_part = magnetic
    across = hx_part[0].ndim - 3
    sideways = across + 1
    bx_hy = subtract(hy_part, below_cell(hy_part, behind_y, across))
    bx_hz = subtract(hz_part, below_cell(hz_part, behind_z, across))
    return (
        subtract(backward_wrap(hz_part, sideways, cosine, sine), backward_open(hy_part)),
        subtract(backward_open(hx_part), bx_hz),
        subtract(bx_hy, backward_wrap(hx_part, sideways, cosine, sine)),
    )


def relax(couple, change, retain, factor):
    return (retain * couple[0] + factor * change[0], retain * couple[1] + factor * change[1])


def coefficients(material, permittivity, absorption_peak, depth):
    height = jnp.arange(depth, dtype=jnp.float32)
    low_depth = jnp.maximum(PML - height, 0.0) / PML
    high_depth = jnp.maximum(height - (depth - 1 - PML), 0.0) / PML
    conduct = absorption_peak[0] * (low_depth**3 + high_depth**3)
    half_mag = conduct * (0.5 * TIME_STEP)
    h_retain = (1.0 - half_mag) / (1.0 + half_mag)
    h_factor = -TIME_STEP / (1.0 + half_mag)
    relative = jnp.zeros(material.shape, jnp.float32)
    for level in range(NMAT):
        relative = relative + jnp.where(material == level, permittivity[level], 0.0)
    half_ele = conduct * (0.5 * TIME_STEP) / relative
    e_retain = (1.0 - half_ele) / (1.0 + half_ele)
    e_factor = TIME_STEP / relative / (1.0 + half_ele)
    return (e_retain, e_factor, h_retain, h_factor)


def split_plane(stacked, member):
    return (stacked[:, 2 * member : 2 * member + 1], stacked[:, 2 * member + 1 : 2 * member + 2])


def on_device(
    bloch_index,
    material,
    permittivity,
    absorption_peak,
    source_sheet,
    waveform,
    electric_in,
    magnetic_in,
):
    points = bloch_index.shape[0]
    rows, width, depth = material.shape
    e_retain, e_factor, h_retain, h_factor = coefficients(
        material, permittivity, absorption_peak, depth
    )
    plane = (jnp.arange(depth) == PML + 2).astype(jnp.float32)
    monitor = PML + 6
    angles = 2.0 * jnp.pi * bloch_index.astype(jnp.float32) / MPHASE
    cos_x = jnp.cos(angles[:, 0]).reshape(points, 1, 1, 1)
    sin_x = jnp.sin(angles[:, 0]).reshape(points, 1, 1, 1)
    cos_y = jnp.cos(angles[:, 1]).reshape(points, 1, 1, 1)
    sin_y = jnp.sin(angles[:, 1]).reshape(points, 1, 1, 1)
    slab = lax.axis_index("sp")
    slabs = lax.axis_size("sp")
    at_end = slab == slabs - 1
    at_start = slab == 0
    end_cos = jnp.where(at_end, cos_x, 1.0)
    end_sin = jnp.where(at_end, sin_x, 0.0)
    start_cos = jnp.where(at_start, cos_x, 1.0)
    start_sin = jnp.where(at_start, -sin_x, 0.0)
    sheet = (source_sheet[:, 0][..., None] * plane, source_sheet[:, 1][..., None] * plane)
    total_points = points * lax.axis_size("ka")
    cells_plane = rows * slabs * width

    def advance(fields, drive):
        electric, magnetic = fields
        front_plane = jnp.stack(
            [
                electric[1][0][:, 0],
                electric[1][1][:, 0],
                electric[2][0][:, 0],
                electric[2][1][:, 0],
            ],
            1,
        )
        received = shifted_2(front_plane, "sp", -1)
        beyond_y = rotate(split_plane(received, 0), end_cos, end_sin)
        beyond_z = rotate(split_plane(received, 1), end_cos, end_sin)
        change = electric_curl(electric, beyond_y, beyond_z, cos_y, sin_y)
        magnetic = tuple(
            (
                relax(couple, change_part, h_retain, h_factor)
                for couple, change_part in zip(magnetic, change)
            )
        )
        back_plane = jnp.stack(
            [
                magnetic[1][0][:, rows - 1],
                magnetic[1][1][:, rows - 1],
                magnetic[2][0][:, rows - 1],
                magnetic[2][1][:, rows - 1],
            ],
            1,
        )
        behind = shifted_2(back_plane, "sp", 1)
        behind_y = rotate(split_plane(behind, 0), start_cos, start_sin)
        behind_z = rotate(split_plane(behind, 1), start_cos, start_sin)
        change = magnetic_curl(magnetic, behind_y, behind_z, cos_y, sin_y)
        first_change = (change[0][0] - drive * sheet[0], change[0][1] - drive * sheet[1])
        change = (first_change, change[1], change[2])
        electric = tuple(
            (
                relax(couple, change_part, e_retain, e_factor)
                for couple, change_part in zip(electric, change)
            )
        )
        return (electric, magnetic)

    def snapshot(fields, index):
        fields = lax.fori_loop(
            0,
            INTERVAL,
            lambda inner, held: advance(held, waveform[index * INTERVAL + inner]),
            fields,
        )
        electric = fields[0]
        power = (
            electric[0][0][..., monitor] ** 2
            + electric[0][1][..., monitor] ** 2
            + electric[1][0][..., monitor] ** 2
            + electric[1][1][..., monitor] ** 2
        )
        partial_value = jnp.sum(power, (1, 2)) / cells_plane
        return (fields, partial_value)

    electric_wide = electric_in.astype(jnp.float32)
    magnetic_wide = magnetic_in.astype(jnp.float32)
    start_e = tuple(
        ((electric_wide[:, 2 * member], electric_wide[:, 2 * member + 1]) for member in range(3))
    )
    start_h = tuple(
        ((magnetic_wide[:, 2 * member], magnetic_wide[:, 2 * member + 1]) for member in range(3))
    )
    final, reports = lax.scan(snapshot, (start_e, start_h), jnp.arange(NSNAP))
    reflected = lax.psum(jnp.transpose(reports), "sp")
    reflected_mean = lax.psum(jnp.sum(reflected, 0) / total_points, "ka")
    electric, magnetic = final
    electric_out = jnp.stack([values for couple in electric for values in couple], 1)
    magnetic_out = jnp.stack([values for couple in magnetic for values in couple], 1)
    return (electric_out, magnetic_out, reflected, reflected_mean)


def solution(mesh):
    in_specs = (
        P("ka", None),
        P("sp", None, None),
        P(),
        P(),
        P("ka", None, "sp", None),
        P(),
        P("ka", None, "sp", None, None),
        P("ka", None, "sp", None, None),
    )
    out_specs = (
        P("ka", None, "sp", None, None),
        P("ka", None, "sp", None, None),
        P("ka", None),
        P(),
    )
    return jax.shard_map(
        on_device, mesh=mesh, in_specs=in_specs, out_specs=out_specs, check_vma=False
    )
```

profile of v0, /device:TPU:0, one launch (start us, length us, event | category | flops | bytes accessed | tf_op | source)
XLA Modules:
  0.0 468.7 jit_solution(13137554951830633101)
XLA Ops:
  6.1 3.2 multiply_divide_fusion
  13.5 415.4 %while.90 = (s32[]{:T(128)}, f32[1,16,64,128]{3,2,1,0:T(8,128)S(1)}, f32[1,16,64,128]{3,2,1,0:T(8,128)S(1)}, f32[1,16,64,128]{3,2,1,0:T(8,128)S(1)}, f32[1,16,64...) while((s32[]{:T(128)}, ...), condition=%wide.region_4.5_spmd.clone.clone, body=%wide.region_0.4_spmd.clone.clone.sunk | while | flops 21113380 | bytes 123783040 | solution.py:239
  17.4 196.4 %while.91 = (s32[]{:T(128)}, f32[1,16,64,128]{3,2,1,0:T(8,128)S(1)}, f32[1,16,64,128]{3,2,1,0:T(8,128)S(1)}, f32[1,16,64,128]{3,2,1,0:T(8,128)S(1)}, f32[1,16,64...) while((s32[]{:T(128)}, ...), condition=%wide.region_2.2_spmd, body=%wide.region_1.1_spmd.sunk | while | flops 20840868 | bytes 118443480 | solution.py:215
  19.0 3.1 collective-permute-start
  40.9 2.8 fusion.98
  53.1 2.2 collective-permute-done.1
  79.1 2.8 fusion.98
  118.7 2.8 fusion.98
  131.0 2.0 collective-permute-done.1
  156.8 2.8 fusion.98
  196.4 2.8 fusion.98
  208.8 2.0 collective-permute-done.1
  225.8 194.9 %while.91 = (s32[]{:T(128)}, f32[1,16,64,128]{3,2,1,0:T(8,128)S(1)}, f32[1,16,64,128]{3,2,1,0:T(8,128)S(1)}, f32[1,16,64,128]{3,2,1,0:T(8,128)S(1)}, f32[1,16,64...) while((s32[]{:T(128)}, ...), condition=%wide.region_2.2_spmd, body=%wide.region_1.1_spmd.sunk | while | flops 20840868 | bytes 118443480 | solution.py:215
  246.6 2.8 fusion.98
  266.3 2.5 collective-permute-start
  287.6 2.8 fusion.98
  299.8 2.2 collective-permute-done.1
  325.6 2.8 fusion.98
  334.9 1.9 collective-permute-start.1
  365.4 2.8 fusion.98
  377.6 2.1 collective-permute-done.1
  403.4 2.8 fusion.98
  433.8 4.9 %psum.14 = f32[1,2]{1,0:T(1,128)S(1)} all-reduce(f32[1,2]{1,0:T(1,128)S(1)} %bitcast.218), channel_id=1, replica_groups=mesh['ka'=16,'sp'=2] {'sp'}, use_global_device_ids=true, to_apply=%region_5.6 | all-reduce | flops 2 | bytes 16 | tf_op jit(solution)/shard_map/psum | solution.py:240
  438.7 30.0 %psum.15 = f32[2]{0:T(128)} all-reduce(f32[2]{0:T(128)S(1)} %multiply_bitcast_fusion), channel_id=1, replica_groups=mesh['ka'=16,'sp'=2] {'ka'}, use_global_device_ids=true, to_apply=%region_6.7 | all-reduce | flops 2 | bytes 16 | tf_op jit(solution)/shard_map/psum | solution.py:241
  (1494 shorter events, 370.5 us)
Async XLA Ops:
  19.0 21.8 %collective-permute-start = (f32[1,4,64,128]{3,2,1,0:T(8,128)S(1)}, f32[1,4,64,128]{3,2,1,0:T(8,128)S(1)}, u32[]{:S(2)}, u32[]{:S(2)}) collective-permute-start(f32[1,4,64,128]{3,2,1,0:T(8,128)S(1)} %pad_maximum_fusion.12), channel_id=1, source_target_pairs={{0,1},{1,0},{2,3},{3,2},{4,5},{5,4},{6,7},{7,6},{8,9},{9,8},{10,11... | collective-permute-start | bytes 393224 | tf_op jit(solution)/shard_map/while/body/eval_jaxpr/while/body/eval_jaxpr/ppermute | solution.py:19
  46.6 11.0 %copy-start.3 = (f32[1,16,64,128]{3,2,1,0:T(8,128)}, f32[1,16,64,128]{3,2,1,0:T(8,128)S(1)}, u32[]{:S(2)}) copy-start(f32[1,16,64,128]{3,2,1,0:T(8,128)S(1)} %fusion.97) | copy-start | bytes 1572868 | tf_op jit(solution)/shard_map/while/body/eval_jaxpr/while
  50.2 5.0 %collective-permute-start.1 = (f32[1,4,64,128]{3,2,1,0:T(8,128)S(1)}, f32[1,4,64,128]{3,2,1,0:T(8,128)S(1)}, u32[]{:S(2)}, u32[]{:S(2)}) collective-permute-start(f32[1,4,64,128]{3,2,1,0:T(8,128)S(1)} %pad_maximum_fusion.13), channel_id=1, source_target_pairs={{0,1},{1,0},{2,3},{3,2},{4,5},{5,4},{6,7},{7,6},{8,9},{9,8},{10,11... | collective-permute-start | bytes 393224 | tf_op jit(solution)/shard_map/while/body/eval_jaxpr/while/body/eval_jaxpr/ppermute | solution.py:19
  59.9 19.1 %collective-permute-start = (f32[1,4,64,128]{3,2,1,0:T(8,128)S(1)}, f32[1,4,64,128]{3,2,1,0:T(8,128)S(1)}, u32[]{:S(2)}, u32[]{:S(2)}) collective-permute-start(f32[1,4,64,128]{3,2,1,0:T(8,128)S(1)} %pad_maximum_fusion.12), channel_id=1, source_target_pairs={{0,1},{1,0},{2,3},{3,2},{4,5},{5,4},{6,7},{7,6},{8,9},{9,8},{10,11... | collective-permute-start | bytes 393224 | tf_op jit(solution)/shard_map/while/body/eval_jaxpr/while/body/eval_jaxpr/ppermute | solution.py:19
  84.7 11.0 %copy-start.3 = (f32[1,16,64,128]{3,2,1,0:T(8,128)}, f32[1,16,64,128]{3,2,1,0:T(8,128)S(1)}, u32[]{:S(2)}) copy-start(f32[1,16,64,128]{3,2,1,0:T(8,128)S(1)} %fusion.97) | copy-start | bytes 1572868 | tf_op jit(solution)/shard_map/while/body/eval_jaxpr/while
  88.4 5.0 %collective-permute-start.1 = (f32[1,4,64,128]{3,2,1,0:T(8,128)S(1)}, f32[1,4,64,128]{3,2,1,0:T(8,128)S(1)}, u32[]{:S(2)}, u32[]{:S(2)}) collective-permute-start(f32[1,4,64,128]{3,2,1,0:T(8,128)S(1)} %pad_maximum_fusion.13), channel_id=1, source_target_pairs={{0,1},{1,0},{2,3},{3,2},{4,5},{5,4},{6,7},{7,6},{8,9},{9,8},{10,11... | collective-permute-start | bytes 393224 | tf_op jit(solution)/shard_map/while/body/eval_jaxpr/while/body/eval_jaxpr/ppermute | solution.py:19
  98.1 20.6 %collective-permute-start = (f32[1,4,64,128]{3,2,1,0:T(8,128)S(1)}, f32[1,4,64,128]{3,2,1,0:T(8,128)S(1)}, u32[]{:S(2)}, u32[]{:S(2)}) collective-permute-start(f32[1,4,64,128]{3,2,1,0:T(8,128)S(1)} %pad_maximum_fusion.12), channel_id=1, source_target_pairs={{0,1},{1,0},{2,3},{3,2},{4,5},{5,4},{6,7},{7,6},{8,9},{9,8},{10,11... | collective-permute-start | bytes 393224 | tf_op jit(solution)/shard_map/while/body/eval_jaxpr/while/body/eval_jaxpr/ppermute | solution.py:19
  128.0 5.0 %collective-permute-start.1 = (f32[1,4,64,128]{3,2,1,0:T(8,128)S(1)}, f32[1,4,64,128]{3,2,1,0:T(8,128)S(1)}, u32[]{:S(2)}, u32[]{:S(2)}) collective-permute-start(f32[1,4,64,128]{3,2,1,0:T(8,128)S(1)} %pad_maximum_fusion.13), channel_id=1, source_target_pairs={{0,1},{1,0},{2,3},{3,2},{4,5},{5,4},{6,7},{7,6},{8,9},{9,8},{10,11... | collective-permute-start | bytes 393224 | tf_op jit(solution)/shard_map/while/body/eval_jaxpr/while/body/eval_jaxpr/ppermute | solution.py:19
  137.7 19.1 %collective-permute-start = (f32[1,4,64,128]{3,2,1,0:T(8,128)S(1)}, f32[1,4,64,128]{3,2,1,0:T(8,128)S(1)}, u32[]{:S(2)}, u32[]{:S(2)}) collective-permute-start(f32[1,4,64,128]{3,2,1,0:T(8,128)S(1)} %pad_maximum_fusion.12), channel_id=1, source_target_pairs={{0,1},{1,0},{2,3},{3,2},{4,5},{5,4},{6,7},{7,6},{8,9},{9,8},{10,11... | collective-permute-start | bytes 393224 | tf_op jit(solution)/shard_map/while/body/eval_jaxpr/while/body/eval_jaxpr/ppermute | solution.py:19
  166.1 5.0 %collective-permute-start.1 = (f32[1,4,64,128]{3,2,1,0:T(8,128)S(1)}, f32[1,4,64,128]{3,2,1,0:T(8,128)S(1)}, u32[]{:S(2)}, u32[]{:S(2)}) collective-permute-start(f32[1,4,64,128]{3,2,1,0:T(8,128)S(1)} %pad_maximum_fusion.13), channel_id=1, source_target_pairs={{0,1},{1,0},{2,3},{3,2},{4,5},{5,4},{6,7},{7,6},{8,9},{9,8},{10,11... | collective-permute-start | bytes 393224 | tf_op jit(solution)/shard_map/while/body/eval_jaxpr/while/body/eval_jaxpr/ppermute | solution.py:19
  175.8 20.6 %collective-permute-start = (f32[1,4,64,128]{3,2,1,0:T(8,128)S(1)}, f32[1,4,64,128]{3,2,1,0:T(8,128)S(1)}, u32[]{:S(2)}, u32[]{:S(2)}) collective-permute-start(f32[1,4,64,128]{3,2,1,0:T(8,128)S(1)} %pad_maximum_fusion.12), channel_id=1, source_target_pairs={{0,1},{1,0},{2,3},{3,2},{4,5},{5,4},{6,7},{7,6},{8,9},{9,8},{10,11... | collective-permute-start | bytes 393224 | tf_op jit(solution)/shard_map/while/body/eval_jaxpr/while/body/eval_jaxpr/ppermute | solution.py:19
  205.7 5.0 %collective-permute-start.1 = (f32[1,4,64,128]{3,2,1,0:T(8,128)S(1)}, f32[1,4,64,128]{3,2,1,0:T(8,128)S(1)}, u32[]{:S(2)}, u32[]{:S(2)}) collective-permute-start(f32[1,4,64,128]{3,2,1,0:T(8,128)S(1)} %pad_maximum_fusion.13), channel_id=1, source_target_pairs={{0,1},{1,0},{2,3},{3,2},{4,5},{5,4},{6,7},{7,6},{8,9},{9,8},{10,11... | collective-permute-start | bytes 393224 | tf_op jit(solution)/shard_map/while/body/eval_jaxpr/while/body/eval_jaxpr/ppermute | solution.py:19
  227.5 19.1 %collective-permute-start = (f32[1,4,64,128]{3,2,1,0:T(8,128)S(1)}, f32[1,4,64,128]{3,2,1,0:T(8,128)S(1)}, u32[]{:S(2)}, u32[]{:S(2)}) collective-permute-start(f32[1,4,64,128]{3,2,1,0:T(8,128)S(1)} %pad_maximum_fusion.12), channel_id=1, source_target_pairs={{0,1},{1,0},{2,3},{3,2},{4,5},{5,4},{6,7},{7,6},{8,9},{9,8},{10,11... | collective-permute-start | bytes 393224 | tf_op jit(solution)/shard_map/while/body/eval_jaxpr/while/body/eval_jaxpr/ppermute | solution.py:19
  252.3 11.7 %copy-start.3 = (f32[1,16,64,128]{3,2,1,0:T(8,128)}, f32[1,16,64,128]{3,2,1,0:T(8,128)S(1)}, u32[]{:S(2)}) copy-start(f32[1,16,64,128]{3,2,1,0:T(8,128)S(1)} %fusion.97) | copy-start | bytes 1572868 | tf_op jit(solution)/shard_map/while/body/eval_jaxpr/while
  255.9 5.7 %collective-permute-start.1 = (f32[1,4,64,128]{3,2,1,0:T(8,128)S(1)}, f32[1,4,64,128]{3,2,1,0:T(8,128)S(1)}, u32[]{:S(2)}, u32[]{:S(2)}) collective-permute-start(f32[1,4,64,128]{3,2,1,0:T(8,128)S(1)} %pad_maximum_fusion.13), channel_id=1, source_target_pairs={{0,1},{1,0},{2,3},{3,2},{4,5},{5,4},{6,7},{7,6},{8,9},{9,8},{10,11... | collective-permute-start | bytes 393224 | tf_op jit(solution)/shard_map/while/body/eval_jaxpr/while/body/eval_jaxpr/ppermute | solution.py:19
  266.3 21.3 %collective-permute-start = (f32[1,4,64,128]{3,2,1,0:T(8,128)S(1)}, f32[1,4,64,128]{3,2,1,0:T(8,128)S(1)}, u32[]{:S(2)}, u32[]{:S(2)}) collective-permute-start(f32[1,4,64,128]{3,2,1,0:T(8,128)S(1)} %pad_maximum_fusion.12), channel_id=1, source_target_pairs={{0,1},{1,0},{2,3},{3,2},{4,5},{5,4},{6,7},{7,6},{8,9},{9,8},{10,11... | collective-permute-start | bytes 393224 | tf_op jit(solution)/shard_map/while/body/eval_jaxpr/while/body/eval_jaxpr/ppermute | solution.py:19
  296.9 5.0 %collective-permute-start.1 = (f32[1,4,64,128]{3,2,1,0:T(8,128)S(1)}, f32[1,4,64,128]{3,2,1,0:T(8,128)S(1)}, u32[]{:S(2)}, u32[]{:S(2)}) collective-permute-start(f32[1,4,64,128]{3,2,1,0:T(8,128)S(1)} %pad_maximum_fusion.13), channel_id=1, source_target_pairs={{0,1},{1,0},{2,3},{3,2},{4,5},{5,4},{6,7},{7,6},{8,9},{9,8},{10,11... | collective-permute-start | bytes 393224 | tf_op jit(solution)/shard_map/while/body/eval_jaxpr/while/body/eval_jaxpr/ppermute | solution.py:19
  306.6 19.0 %collective-permute-start = (f32[1,4,64,128]{3,2,1,0:T(8,128)S(1)}, f32[1,4,64,128]{3,2,1,0:T(8,128)S(1)}, u32[]{:S(2)}, u32[]{:S(2)}) collective-permute-start(f32[1,4,64,128]{3,2,1,0:T(8,128)S(1)} %pad_maximum_fusion.12), channel_id=1, source_target_pairs={{0,1},{1,0},{2,3},{3,2},{4,5},{5,4},{6,7},{7,6},{8,9},{9,8},{10,11... | collective-permute-start | bytes 393224 | tf_op jit(solution)/shard_map/while/body/eval_jaxpr/while/body/eval_jaxpr/ppermute | solution.py:19
  334.9 5.0 %collective-permute-start.1 = (f32[1,4,64,128]{3,2,1,0:T(8,128)S(1)}, f32[1,4,64,128]{3,2,1,0:T(8,128)S(1)}, u32[]{:S(2)}, u32[]{:S(2)}) collective-permute-start(f32[1,4,64,128]{3,2,1,0:T(8,128)S(1)} %pad_maximum_fusion.13), channel_id=1, source_target_pairs={{0,1},{1,0},{2,3},{3,2},{4,5},{5,4},{6,7},{7,6},{8,9},{9,8},{10,11... | collective-permute-start | bytes 393224 | tf_op jit(solution)/shard_map/while/body/eval_jaxpr/while/body/eval_jaxpr/ppermute | solution.py:19
  344.6 20.7 %collective-permute-start = (f32[1,4,64,128]{3,2,1,0:T(8,128)S(1)}, f32[1,4,64,128]{3,2,1,0:T(8,128)S(1)}, u32[]{:S(2)}, u32[]{:S(2)}) collective-permute-start(f32[1,4,64,128]{3,2,1,0:T(8,128)S(1)} %pad_maximum_fusion.12), channel_id=1, source_target_pairs={{0,1},{1,0},{2,3},{3,2},{4,5},{5,4},{6,7},{7,6},{8,9},{9,8},{10,11... | collective-permute-start | bytes 393224 | tf_op jit(solution)/shard_map/while/body/eval_jaxpr/while/body/eval_jaxpr/ppermute | solution.py:19
  374.7 5.0 %collective-permute-start.1 = (f32[1,4,64,128]{3,2,1,0:T(8,128)S(1)}, f32[1,4,64,128]{3,2,1,0:T(8,128)S(1)}, u32[]{:S(2)}, u32[]{:S(2)}) collective-permute-start(f32[1,4,64,128]{3,2,1,0:T(8,128)S(1)} %pad_maximum_fusion.13), channel_id=1, source_target_pairs={{0,1},{1,0},{2,3},{3,2},{4,5},{5,4},{6,7},{7,6},{8,9},{9,8},{10,11... | collective-permute-start | bytes 393224 | tf_op jit(solution)/shard_map/while/body/eval_jaxpr/while/body/eval_jaxpr/ppermute | solution.py:19
  384.4 19.0 %collective-permute-start = (f32[1,4,64,128]{3,2,1,0:T(8,128)S(1)}, f32[1,4,64,128]{3,2,1,0:T(8,128)S(1)}, u32[]{:S(2)}, u32[]{:S(2)}) collective-permute-start(f32[1,4,64,128]{3,2,1,0:T(8,128)S(1)} %pad_maximum_fusion.12), channel_id=1, source_target_pairs={{0,1},{1,0},{2,3},{3,2},{4,5},{5,4},{6,7},{7,6},{8,9},{9,8},{10,11... | collective-permute-start | bytes 393224 | tf_op jit(solution)/shard_map/while/body/eval_jaxpr/while/body/eval_jaxpr/ppermute | solution.py:19
  412.7 5.0 %collective-permute-start.1 = (f32[1,4,64,128]{3,2,1,0:T(8,128)S(1)}, f32[1,4,64,128]{3,2,1,0:T(8,128)S(1)}, u32[]{:S(2)}, u32[]{:S(2)}) collective-permute-start(f32[1,4,64,128]{3,2,1,0:T(8,128)S(1)} %pad_maximum_fusion.13), channel_id=1, source_target_pairs={{0,1},{1,0},{2,3},{3,2},{4,5},{5,4},{6,7},{7,6},{8,9},{9,8},{10,11... | collective-permute-start | bytes 393224 | tf_op jit(solution)/shard_map/while/body/eval_jaxpr/while/body/eval_jaxpr/ppermute | solution.py:19
  438.7 30.0 %copy-start.60 = (f32[1,2]{1,0:T(1,128)}, f32[1,2]{1,0:T(1,128)S(1)}, u32[]{:S(2)}) copy-start(f32[1,2]{1,0:T(1,128)S(1)} %psum.14) | copy-start | bytes 28
  (416 other events, 1818.8 us)
where the time goes:
time: 474 us; the launch traced here: 469 us
  local copies, waits for them, and re-layouts  230 us (49%)
  other arithmetic  153 us (32%)
  blocking collectives  34.9 us (7%)
  starting transfers between devices  23 us (5%)
  waiting for transfers between devices  13.4 us (3%)
  loops' own time  9.35 us (2%)
    slice x280, local copies, waits for them, and re-layouts, roll_couple(): return tuple((jnp.roll(values, amount, axis=along) for values in couple))  160 us
    add x60, other arithmetic, relax(): retain * couple[1] + factor * change[1]  70.4 us
    add x60, other arithmetic, relax(): retain * couple[0] + factor * change[0]  54.8 us
    psum x1, blocking collectives, on_device(): reflected_mean = lax.psum(jnp.sum(reflected, 0) / total_points, 'ka')  30 us
    ppermute x20, starting transfers between devices, shifted_2(): return lax.ppermute(value, axis, pairs)  23 us
    dynamic_slice x10, local copies, waits for them, and re-layouts, snapshot(): waveform[index * INTERVAL + inner]  13.7 us
    ppermute x20, waiting for transfers between devices, shifted_2(): return lax.ppermute(value, axis, pairs)  13.4 us
    while x8, local copies, waits for them, and re-layouts, snapshot(): lax.fori_loop(0, INTERVAL, lambda inner, held: advance(held, waveform[ind...  11.1 us
  transfers between devices with their start and end apart: 20, of which 10 were waited for; matrix products, arithmetic and copies ran while one was open for 45% of the time, Pallas kernels for 0%

commit v1 on v0

v1 whole, which is shorter than its diff:
```python
import functools

import jax
import jax.numpy as jnp
from jax import lax
from jax.experimental import pallas as pl
from jax.experimental.pallas import tpu as pltpu
from jax.sharding import PartitionSpec as P

PML = 16
INTERVAL = 5
MPHASE = 64
NMAT = 3
TIME_STEP = 0.5
MESH = pl.DeviceIdType.MESH


def rotate(couple, cosine, sine):
    return (couple[0] * cosine - couple[1] * sine, couple[0] * sine + couple[1] * cosine)


def minus(left, right):
    return (left[0] - right[0], left[1] - right[1])


def plus(left, right):
    return (left[0] + right[0], left[1] + right[1])


def relax(couple, change, keep, gain):
    return tuple(keep * c + gain * d for c, d in zip(couple, change))


def kernel(
    bloch_ref,
    perm_ref,
    peak_ref,
    wave_ref,
    material_ref,
    sheet_ref,
    e_in,
    h_in,
    e_ref,
    h_ref,
    report_ref,
    keep_ref,
    gain_ref,
    drive_ref,
    out_e,
    out_w,
    got_e,
    got_w,
    send_e,
    send_w,
    recv_e,
    recv_w,
):
    rows, width, depth = material_ref.shape
    steps = wave_ref.shape[0]
    slabs = lax.axis_size("sp")
    slab = lax.axis_index("sp")
    upper = lax.rem(slab + 1, slabs)
    lower = lax.rem(slab + slabs - 1, slabs)

    barrier = pltpu.get_barrier_semaphore()
    for other in (lower, upper):
        pl.semaphore_signal(barrier, inc=1, device_id={"sp": other}, device_id_type=MESH)

    height = lax.broadcasted_iota(jnp.int32, (8, depth), 1).astype(jnp.float32)
    low_depth = jnp.maximum(PML - height, 0.0) / PML
    high_depth = jnp.maximum(height - (depth - 1 - PML), 0.0) / PML
    conduct = peak_ref[0] * (
        low_depth * low_depth * low_depth + high_depth * high_depth * high_depth
    )
    half_mag = conduct * (0.5 * TIME_STEP)
    h_keep = ((1.0 - half_mag) / (1.0 + half_mag))[0:1]
    h_gain = (-TIME_STEP / (1.0 + half_mag))[0:1]
    tables = []
    for level in range(NMAT):
        relative = jnp.full((8, depth), perm_ref[level], jnp.float32)
        half_ele = conduct * (0.5 * TIME_STEP) / relative
        tables.append(
            (
                ((1.0 - half_ele) / (1.0 + half_ele))[0:1],
                (TIME_STEP / relative / (1.0 + half_ele))[0:1],
            )
        )

    def trig(member):
        angle = jnp.full((8, depth), bloch_ref[0, member], jnp.int32).astype(jnp.float32)
        angle = 2.0 * jnp.pi * angle / MPHASE
        return jnp.cos(angle)[0:1], jnp.sin(angle)[0:1]

    cos_x, sin_x = trig(0)
    cos_y, sin_y = trig(1)
    at_end = (slab == slabs - 1).astype(jnp.float32)
    at_start = (slab == 0).astype(jnp.float32)
    end_cos = at_end * cos_x + (1.0 - at_end)
    end_sin = at_end * sin_x
    start_cos = at_start * cos_x + (1.0 - at_start)
    start_sin = -at_start * sin_x

    lane = lax.broadcasted_iota(jnp.int32, (width, depth), 1)
    last_lane = lane == depth - 1
    first_lane = lane == 0
    sub = lax.broadcasted_iota(jnp.int32, (8, depth), 0)

    def above_z(couple):
        return tuple(jnp.where(last_lane, 0.0, pltpu.roll(v, depth - 1, 1)) for v in couple)

    def below_z(couple):
        return tuple(jnp.where(first_lane, 0.0, pltpu.roll(v, 1, 1)) for v in couple)

    def above_y(couple):
        moved = tuple(pltpu.roll(v, width - 1, 0) for v in couple)
        tail = tuple(v[width - 8 :] for v in moved)
        turned = rotate(tail, cos_y, sin_y)
        return tuple(
            jnp.concatenate([v[: width - 8], jnp.where(sub == 7, r, w)], axis=0)
            for v, r, w in zip(moved, turned, tail)
        )

    def below_y(couple):
        moved = tuple(pltpu.roll(v, 1, 0) for v in couple)
        head = tuple(v[:8] for v in moved)
        turned = rotate(head, cos_y, -sin_y)
        return tuple(
            jnp.concatenate([jnp.where(sub == 0, r, w), v[8:]], axis=0)
            for v, r, w in zip(moved, turned, head)
        )

    def get(ref, member, x):
        return (ref[0, 2 * member, x], ref[0, 2 * member + 1, x])

    def put(ref, member, x, couple):
        ref[0, 2 * member, x] = couple[0]
        ref[0, 2 * member + 1, x] = couple[1]

    def get_plane(ref, slot, member):
        return (ref[slot, 2 * member], ref[slot, 2 * member + 1])

    def put_plane(ref, slot, member, couple):
        ref[slot, 2 * member] = couple[0]
        ref[slot, 2 * member + 1] = couple[1]

    def hx_plane(x):
        ey, ez = get(e_ref, 1, x), get(e_ref, 2, x)
        change = minus(minus(above_y(ez), ez), minus(above_z(ey), ey))
        put(h_ref, 0, x, relax(get(h_ref, 0, x), change, h_keep, h_gain))

    def h_plane(x, carry):
        hx_plane(x)
        ex, ey, ez = get(e_ref, 0, x), get(e_ref, 1, x), get(e_ref, 2, x)
        dx_ez = minus(get(e_ref, 2, x + 1), ez)
        dx_ey = minus(get(e_ref, 1, x + 1), ey)
        change = minus(minus(above_z(ex), ex), dx_ez)
        put(h_ref, 1, x, relax(get(h_ref, 1, x), change, h_keep, h_gain))
        change = minus(dx_ey, minus(above_y(ex), ex))
        put(h_ref, 2, x, relax(get(h_ref, 2, x), change, h_keep, h_gain))
        return carry

    def partial_h(slot):
        x = rows - 1
        ex, ey, ez = get(e_ref, 0, x), get(e_ref, 1, x), get(e_ref, 2, x)
        change = plus(minus(above_z(ex), ex), ez)
        put_plane(out_w, slot, 0, relax(get(h_ref, 1, x), change, h_keep, h_gain))
        change = minus(minus(ex, above_y(ex)), ey)
        put_plane(out_w, slot, 1, relax(get(h_ref, 2, x), change, h_keep, h_gain))

    def complete_h(slot):
        x = rows - 1
        beyond_y = rotate(get_plane(got_e, slot, 0), end_cos, end_sin)
        beyond_z = rotate(get_plane(got_e, slot, 1), end_cos, end_sin)
        w_y, w_z = get_plane(out_w, slot, 0), get_plane(out_w, slot, 1)
        put(h_ref, 1, x, tuple(w - h_gain * b for w, b in zip(w_y, beyond_z)))
        put(h_ref, 2, x, tuple(w + h_gain * b for w, b in zip(w_z, beyond_y)))

    def e_update(x, drive, hy_prev, hz_prev):
        hx, hy, hz = get(h_ref, 0, x), get(h_ref, 1, x), get(h_ref, 2, x)
        keep, gain = keep_ref[x], gain_ref[x]
        change = minus(minus(hz, below_y(hz)), minus(hy, below_z(hy)))
        change = (change[0] - drive * drive_ref[0, x], change[1] - drive * drive_ref[1, x])
        put(e_ref, 0, x, relax(get(e_ref, 0, x), change, keep, gain))
        change = minus(minus(hx, below_z(hx)), minus(hz, hz_prev))
        ey = relax(get(e_ref, 1, x), change, keep, gain)
        put(e_ref, 1, x, ey)
        change = minus(minus(hy, hy_prev), minus(hx, below_y(hx)))
        ez = relax(get(e_ref, 2, x), change, keep, gain)
        put(e_ref, 2, x, ez)
        return ey, ez

    def e_first(slot, drive):
        ey, ez = get(e_ref, 1, 0), get(e_ref, 2, 0)
        turned_y = rotate(get_plane(got_w, slot, 0), start_cos, start_sin)
        turned_z = rotate(get_plane(got_w, slot, 1), start_cos, start_sin)
        hy_prev = tuple(w - h_gain * e for w, e in zip(turned_y, ez))
        hz_prev = tuple(w + h_gain * e for w, e in zip(turned_z, ey))
        return e_update(0, drive, hy_prev, hz_prev)

    def copy_e(slot):
        return pltpu.make_async_remote_copy(
            src_ref=out_e.at[slot],
            dst_ref=got_e.at[slot],
            send_sem=send_e.at[slot],
            recv_sem=recv_e.at[slot],
            device_id={"sp": lower},
            device_id_type=MESH,
        )

    def copy_w(slot):
        return pltpu.make_async_remote_copy(
            src_ref=out_w.at[slot],
            dst_ref=got_w.at[slot],
            send_sem=send_w.at[slot],
            recv_sem=recv_w.at[slot],
            device_id={"sp": upper},
            device_id_type=MESH,
        )

    def widen(x, carry):
        for member in range(6):
            e_ref[0, member, x] = e_in[0, member, x].astype(jnp.float32)
            h_ref[0, member, x] = h_in[0, member, x].astype(jnp.float32)
        return carry

    widen(0, 0)
    widen(rows - 1, 0)
    for member in range(2):
        put_plane(out_e, 0, member, get(e_ref, 1 + member, 0))
    partial_h(0)
    pl.semaphore_wait(barrier, 2)
    copy_e(0).start()
    copy_w(0).start()
    lax.fori_loop(1, rows - 1, widen, 0)

    square = lax.broadcasted_iota(jnp.int32, (width, width), 0) == lax.broadcasted_iota(
        jnp.int32, (width, width), 1
    )

    def prepare(x, carry):
        kind = material_ref[x]
        keep, gain = tables[0]
        for level in range(1, NMAT):
            keep = jnp.where(kind == level, tables[level][0], keep)
            gain = jnp.where(kind == level, tables[level][1], gain)
        keep_ref[x] = keep
        gain_ref[x] = gain
        for part in range(2):
            row = sheet_ref[0, part, pl.ds(x, 1), :]
            column = jnp.sum(jnp.where(square, row, 0.0), axis=1, keepdims=True)
            drive_ref[part, x] = jnp.where(lane == PML + 2, column, 0.0)
        return carry

    lax.fori_loop(0, rows, prepare, 0)

    def step(t, carry):
        slot = lax.rem(t, 2)
        later = lax.rem(t + 1, 2)
        drive = wave_ref[t]
        lax.fori_loop(0, rows - 1, h_plane, 0)
        hx_plane(rows - 1)
        copy_w(slot).wait_recv()
        ey, ez = e_first(slot, drive)

        @pl.when(jnp.logical_and(t >= 1, t < steps - 1))
        def _():
            copy_e(later).wait_send()

        @pl.when(t < steps - 1)
        def _():
            put_plane(out_e, later, 0, ey)
            put_plane(out_e, later, 1, ez)
            copy_e(later).start()

        def inner(x, held):
            e_update(x, drive, get(h_ref, 1, x - 1), get(h_ref, 2, x - 1))
            return held

        lax.fori_loop(1, rows - 1, inner, 0)
        copy_e(slot).wait_recv()
        complete_h(slot)
        e_update(rows - 1, drive, get(h_ref, 1, rows - 2), get(h_ref, 2, rows - 2))

        @pl.when(jnp.logical_and(t >= 1, t < steps - 1))
        def _():
            copy_w(later).wait_send()

        @pl.when(t < steps - 1)
        def _():
            partial_h(later)
            copy_w(later).start()

        @pl.when(lax.rem(t + 1, INTERVAL) == 0)
        def _():
            def power(x, total):
                for member in range(4):
                    value = e_ref[0, member, x]
                    total = total + value * value
                return total

            total = lax.fori_loop(0, rows, power, jnp.zeros((width, depth), jnp.float32))
            folded = total[0:8]
            for at in range(8, width, 8):
                folded = folded + total[at : at + 8]
            report_ref[lax.div(t, INTERVAL)] = folded

        return carry

    lax.fori_loop(0, steps, step, 0)
    for t in (steps - 2, steps - 1):
        copy_e(t % 2).wait_send()
        copy_w(t % 2).wait_send()


def one_point(bloch, material, permittivity, peak, sheet, waveform, electric, magnetic):
    rows, width, depth = material.shape
    snaps = waveform.shape[0] // INTERVAL
    smem = pl.BlockSpec(memory_space=pltpu.SMEM)
    vmem = pl.BlockSpec(memory_space=pltpu.VMEM)
    plane = (2, 4, width, depth)
    f32 = jnp.float32
    return pl.pallas_call(
        kernel,
        out_shape=(
            jax.ShapeDtypeStruct(electric.shape, f32),
            jax.ShapeDtypeStruct(magnetic.shape, f32),
            jax.ShapeDtypeStruct((snaps, 8, depth), f32),
        ),
        in_specs=[smem] * 4 + [vmem] * 4,
        out_specs=(vmem, vmem, vmem),
        scratch_shapes=[
            pltpu.VMEM((rows, width, depth), f32),
            pltpu.VMEM((rows, width, depth), f32),
            pltpu.VMEM((2, rows, width, depth), f32),
            pltpu.VMEM(plane, f32),
            pltpu.VMEM(plane, f32),
            pltpu.VMEM(plane, f32),
            pltpu.VMEM(plane, f32),
            pltpu.SemaphoreType.DMA((2,)),
            pltpu.SemaphoreType.DMA((2,)),
            pltpu.SemaphoreType.DMA((2,)),
            pltpu.SemaphoreType.DMA((2,)),
        ],
        compiler_params=pltpu.CompilerParams(
            collective_id=0, has_side_effects=True, vmem_limit_bytes=40 * 1024 * 1024
        ),
    )(bloch, permittivity, peak, waveform, material, sheet, electric, magnetic)


def on_device(
    bloch_index,
    material,
    permittivity,
    absorption_peak,
    source_sheet,
    waveform,
    electric_in,
    magnetic_in,
):
    points = bloch_index.shape[0]
    rows, width, depth = material.shape
    slabs = lax.axis_size("sp")
    results = [
        one_point(
            bloch_index[p : p + 1],
            material,
            permittivity,
            absorption_peak,
            source_sheet[p : p + 1],
            waveform,
            electric_in[p : p + 1],
            magnetic_in[p : p + 1],
        )
        for p in range(points)
    ]
    electric_out = jnp.concatenate([r[0] for r in results], 0)
    magnetic_out = jnp.concatenate([r[1] for r in results], 0)
    reports = jnp.stack([jnp.sum(r[2][:, :, PML + 6], axis=1) for r in results], 0)
    reflected = lax.psum(reports / (rows * slabs * width), "sp")
    total_points = points * lax.axis_size("ka")
    reflected_mean = lax.psum(jnp.sum(reflected, 0) / total_points, "ka")
    return (electric_out, magnetic_out, reflected, reflected_mean)


def solution(mesh):
    in_specs = (
        P("ka", None),
        P("sp", None, None),
        P(),
        P(),
        P("ka", None, "sp", None),
        P(),
        P("ka", None, "sp", None, None),
        P("ka", None, "sp", None, None),
    )
    out_specs = (
        P("ka", None, "sp", None, None),
        P("ka", None, "sp", None, None),
        P("ka", None),
        P(),
    )
    return jax.shard_map(
        on_device, mesh=mesh, in_specs=in_specs, out_specs=out_specs, check_vma=False
    )
```

time: 474 us -> 125 us (0.26); the launches traced: 469 us -> 125 us
  local copies, waits for them, and re-layouts: 230 us -> 13.8 us
  other arithmetic: 153 us -> 0.18 us
  Pallas kernels: 0 us -> 73.4 us
  starting transfers between devices: 23 us -> 0 us
  waiting for transfers between devices: 13.4 us -> 0 us
  loops' own time: 9.35 us -> 0 us
    slice x362 -> x0, local copies, waits for them, and re-layouts: 185 us -> none  [the longest x280 160 us: roll_couple(): return tuple((jnp.roll(values, amount, axis=along) for values in couple))]
    add x120 -> x0, other arithmetic: 125 us -> none  [the longest x60 70.4 us: relax(): retain * couple[1] + factor * change[1]]
    pallas_call x0 -> x1, Pallas kernels: none -> 73.4 us  [one_point(): pl.pallas_call(kernel, out_shape=(jax.ShapeDtypeStruct(electric.shape, f3...]
    ppermute x20 -> x0, starting transfers between devices: 23 us -> none  [shifted_2(): return lax.ppermute(value, axis, pairs)]
    while x820 -> x0, local copies, waits for them, and re-layouts: 21.8 us -> none  [the longest x8 11.1 us: snapshot(): lax.fori_loop(0, INTERVAL, lambda inner, held: advance(held, waveform[ind...]
    dynamic_slice x12 -> x0, local copies, waits for them, and re-layouts: 16.3 us -> none  [the longest x10 13.7 us: snapshot(): waveform[index * INTERVAL + inner]]
    eq x60 -> x0, other arithmetic: 15.1 us -> none  [the longest x10 5.23 us: below_cell(): first = position(couple[0], along) == 0]
    ppermute x20 -> x0, waiting for transfers between devices: 13.4 us -> none  [shifted_2(): return lax.ppermute(value, axis, pairs)]
  transfers between devices with their start and end apart: 20 -> 0, of which waited for: 10 -> 0; matrix products, arithmetic and copies ran while one was open for 45% -> 0% of each run, Pallas kernels for 0% -> 0%
where the time goes in v1:
time: 125 us
  Pallas kernels  73.4 us (59%)
  blocking collectives  36 us (29%)
  local copies, waits for them, and re-layouts  13.8 us (11%)
  between operations  1.31 us (1%)
    pallas_call x1, Pallas kernels, one_point(): pl.pallas_call(kernel, out_shape=(jax.ShapeDtypeStruct(electric.shape, f3...  73.4 us
    psum x1, blocking collectives, on_device(): reflected_mean = lax.psum(jnp.sum(reflected, 0) / total_points, 'ka')  31.1 us
    unnamed x20, local copies, waits for them, and re-layouts  13.8 us
    psum x1, blocking collectives, on_device(): reflected = lax.psum(reports / (rows * slabs * width), 'sp')  4.91 us

profile of v1, /device:TPU:0, one launch (start us, length us, event | category | flops | bytes accessed | tf_op | source)
XLA Modules:
  0.0 124.8 jit_solution(7984787724846871934)
XLA Ops:
  1.3 0.0 copy-start.1
  1.3 1.4 %copy-done.1 = bf16[1,6,16,64,128]{4,3,2,1,0:T(8,128)(2,1)S(1)} copy-done((bf16[1,6,16,64,128]{4,3,2,1,0:T(8,128)(2,1)S(1)}, bf16[1,6,16,64,128]{4,3,2,1,0:T(8,128)(2,1)}, u32[]{:S(2)}) %copy-start.1) | copy-done | bytes 1572888
  2.7 0.0 copy-start.2
  2.7 1.4 %copy-done.2 = bf16[1,6,16,64,128]{4,3,2,1,0:T(8,128)(2,1)S(1)} copy-done((bf16[1,6,16,64,128]{4,3,2,1,0:T(8,128)(2,1)S(1)}, bf16[1,6,16,64,128]{4,3,2,1,0:T(8,128)(2,1)}, u32[]{:S(2)}) %copy-start.2) | copy-done | bytes 1572888
  4.1 0.0 copy-start.3
  4.1 1.0 copy-done.3
  5.1 0.0 copy-start.4
  5.1 0.7 copy-done.4
  5.9 0.0 copy-start.5
  5.9 0.7 copy-done.5
  6.5 0.0 copy-start.6
  6.5 0.7 copy-done.6
  7.2 0.0 copy-start.7
  7.2 0.7 copy-done.7
  7.8 73.4 %shard_map.111 = (f32[1,6,16,64,128]{4,3,2,1,0:T(8,128)S(1)}, f32[1,6,16,64,128]{4,3,2,1,0:T(8,128)S(1)}, f32[2,8,128]{2,1,0:T(8,128)S(1)}) custom-call(s32[1,2]{1,0:T(1,128)S(1)} %copy-done.5, f32[3]{0:T(128)S(1)} %copy-done.6, f32[1]{0:T(128)S(6)} %copy.14.peak_ref, f32[10]{0:T(128)S(1)} %copy-done.7, s32[16,64,128]{2,1,0:T(8,128)S(1)} %copy-done.3, ...), custom_call_target="tpu_custom_call" | custom-call | tf_op jit(solution)/shard_map/pallas_call | solution.py:322
  81.3 0.0 copy-start
  81.3 1.7 %copy-done = f32[1,6,16,64,128]{4,3,2,1,0:T(8,128)} copy-done((f32[1,6,16,64,128]{4,3,2,1,0:T(8,128)}, f32[1,6,16,64,128]{4,3,2,1,0:T(8,128)S(1)}, u32[]{:S(2)}) %copy-start) | copy-done | bytes 3145752
  82.9 0.2 slice_reduce_fusion
  83.1 4.9 %psum.14 = f32[1,2]{1,0:T(1,128)S(1)} all-reduce(f32[1,2]{1,0:T(1,128)S(1)} %multiply_bitcast_fusion.1), channel_id=1, replica_groups=mesh['ka'=16,'sp'=2] {'sp'}, use_global_device_ids=true, to_apply=%region_1.0 | all-reduce | flops 2 | bytes 16 | tf_op jit(solution)/shard_map/psum | solution.py:379
  88.0 0.0 copy-start.8
  88.0 31.1 %psum.15 = f32[2]{0:T(128)} all-reduce(f32[2]{0:T(128)S(1)} %multiply_bitcast_fusion), channel_id=1, replica_groups=mesh['ka'=16,'sp'=2] {'ka'}, use_global_device_ids=true, to_apply=%region_2.0 | all-reduce | flops 2 | bytes 16 | tf_op jit(solution)/shard_map/psum | solution.py:381
  119.2 4.0 %copy.15 = f32[1,6,16,64,128]{4,3,2,1,0:T(8,128)} copy(f32[1,6,16,64,128]{4,3,2,1,0:T(8,128)} %copy-done) | data formatting | bytes 6291456
  123.1 0.0 copy-done.8
  123.1 1.7 %copy.16 = f32[1,6,16,64,128]{4,3,2,1,0:T(8,128)} copy(f32[1,6,16,64,128]{4,3,2,1,0:T(8,128)S(1)} %get-tuple-element.15) | data formatting | bytes 6291456
  (2 shorter events, 0.0 us)
Async XLA Ops:
  1.3 1.4 %copy-start.1 = (bf16[1,6,16,64,128]{4,3,2,1,0:T(8,128)(2,1)S(1)}, bf16[1,6,16,64,128]{4,3,2,1,0:T(8,128)(2,1)}, u32[]{:S(2)}) copy-start(bf16[1,6,16,64,128]{4,3,2,1,0:T(8,128)(2,1)} %e_in.1) | copy-start | bytes 4718596
  2.7 1.4 %copy-start.2 = (bf16[1,6,16,64,128]{4,3,2,1,0:T(8,128)(2,1)S(1)}, bf16[1,6,16,64,128]{4,3,2,1,0:T(8,128)(2,1)}, u32[]{:S(2)}) copy-start(bf16[1,6,16,64,128]{4,3,2,1,0:T(8,128)(2,1)} %h_in.1) | copy-start | bytes 4718596
  4.1 1.0 copy-start.3
  5.1 0.7 copy-start.4
  5.9 0.7 copy-start.5
  6.5 0.7 copy-start.6
  7.2 0.7 copy-start.7
  81.3 1.7 %copy-start = (f32[1,6,16,64,128]{4,3,2,1,0:T(8,128)}, f32[1,6,16,64,128]{4,3,2,1,0:T(8,128)S(1)}, u32[]{:S(2)}) copy-start(f32[1,6,16,64,128]{4,3,2,1,0:T(8,128)S(1)} %get-tuple-element.14) | copy-start | bytes 9437188
  88.0 35.1 %copy-start.8 = (f32[1,2]{1,0:T(1,128)}, f32[1,2]{1,0:T(1,128)S(1)}, u32[]{:S(2)}) copy-start(f32[1,2]{1,0:T(1,128)S(1)} %psum.14) | copy-start | bytes 28

commit v2 on v1

--- a/solution.py
+++ b/solution.py
@@ -1,5 +1,3 @@
-import functools
-
 import jax
 import jax.numpy as jnp
 from jax import lax
@@ -32,6 +30,18 @@
 
 
 def kernel(
+    bloch_in,
+    perm_in,
+    peak_in,
+    wave_in,
+    material_in,
+    sheet_in,
+    e_hbm,
+    h_hbm,
+    e_ref,
+    h_ref,
+    reflected_ref,
+    mean_ref,
     bloch_ref,
     perm_ref,
     peak_ref,
@@ -40,9 +50,8 @@
     sheet_ref,
     e_in,
     h_in,
-    e_ref,
-    h_ref,
     report_ref,
+    got_report,
     keep_ref,
     gain_ref,
     drive_ref,
@@ -54,6 +63,9 @@
     send_w,
     recv_e,
     recv_w,
+    load_sem,
+    send_report,
+    recv_report,
 ):
     rows, width, depth = material_ref.shape
     steps = wave_ref.shape[0]
@@ -62,9 +74,47 @@
     upper = lax.rem(slab + 1, slabs)
     lower = lax.rem(slab + slabs - 1, slabs)
 
+    groups = lax.axis_size("ka")
+    group = lax.axis_index("ka")
+    everyone = groups * slabs
+    me = group * slabs + slab
+
+    def place(at):
+        return {"ka": lax.div(at, slabs), "sp": lax.rem(at, slabs)}
+
+    last_row = rows - 1
+    loads = [
+        pltpu.make_async_copy(src, dst, load_sem.at[at])
+        for at, (src, dst) in enumerate(
+            (
+                (e_hbm.at[0, :, last_row], e_in.at[0, :, last_row]),
+                (h_hbm.at[0, :, last_row], h_in.at[0, :, last_row]),
+                (e_hbm.at[0, :, 0], e_in.at[0, :, 0]),
+                (h_hbm.at[0, :, 0], h_in.at[0, :, 0]),
+                (bloch_in, bloch_ref),
+                (perm_in, perm_ref),
+                (peak_in, peak_ref),
+                (wave_in, wave_ref),
+                (e_hbm.at[0, :, 1:last_row], e_in.at[0, :, 1:last_row]),
+                (h_hbm.at[0, :, 1:last_row], h_in.at[0, :, 1:last_row]),
+                (material_in, material_ref),
+                (sheet_in, sheet_ref),
+            )
+        )
+    ]
+    for load in loads:
+        load.start()
+
     barrier = pltpu.get_barrier_semaphore()
-    for other in (lower, upper):
-        pl.semaphore_signal(barrier, inc=1, device_id={"sp": other}, device_id_type=MESH)
+
+    def greet(offset, carry):
+        other = lax.rem(me + offset, everyone)
+        pl.semaphore_signal(barrier, inc=1, device_id=place(other), device_id_type=MESH)
+        return carry
+
+    lax.fori_loop(1, everyone, greet, 0)
+    for load in loads[4:8]:
+        load.wait()
 
     height = lax.broadcasted_iota(jnp.int32, (8, depth), 1).astype(jnp.float32)
     low_depth = jnp.maximum(PML - height, 0.0) / PML
@@ -223,16 +273,21 @@
             h_ref[0, member, x] = h_in[0, member, x].astype(jnp.float32)
         return carry
 
+    for load in loads[0:4]:
+        load.wait()
+    widen(rows - 1, 0)
+    partial_h(0)
     widen(0, 0)
-    widen(rows - 1, 0)
     for member in range(2):
         put_plane(out_e, 0, member, get(e_ref, 1 + member, 0))
-    partial_h(0)
-    pl.semaphore_wait(barrier, 2)
+    pl.semaphore_wait(barrier, everyone - 1)
+    copy_w(0).start()
     copy_e(0).start()
-    copy_w(0).start()
+    for load in loads[8:]:
+        load.wait()
     lax.fori_loop(1, rows - 1, widen, 0)
 
+    report_ref[...] = jnp.zeros_like(report_ref)
     square = lax.broadcasted_iota(jnp.int32, (width, width), 0) == lax.broadcasted_iota(
         jnp.int32, (width, width), 1
     )
@@ -253,6 +308,12 @@
 
     lax.fori_loop(0, rows, prepare, 0)
 
+    def power(x, total):
+        for member in range(4):
+            value = e_ref[0, member, x]
+            total = total + value * value
+        return total
+
     def step(t, carry):
         slot = lax.rem(t, 2)
         later = lax.rem(t + 1, 2)
@@ -277,6 +338,12 @@
             return held
 
         lax.fori_loop(1, rows - 1, inner, 0)
+
+        @pl.when(lax.rem(t + 1, INTERVAL) == 0)
+        def _():
+            total = lax.fori_loop(0, rows - 1, power, jnp.zeros((width, depth), jnp.float32))
+            report_ref[pl.ds(lax.div(t, INTERVAL), 1)] = jnp.sum(total, axis=0, keepdims=True)
+
         copy_e(slot).wait_recv()
         complete_h(slot)
         e_update(rows - 1, drive, get(h_ref, 1, rows - 2), get(h_ref, 2, rows - 2))
@@ -292,30 +359,55 @@
 
         @pl.when(lax.rem(t + 1, INTERVAL) == 0)
         def _():
-            def power(x, total):
-                for member in range(4):
-                    value = e_ref[0, member, x]
-                    total = total + value * value
-                return total
-
-            total = lax.fori_loop(0, rows, power, jnp.zeros((width, depth), jnp.float32))
-            folded = total[0:8]
-            for at in range(8, width, 8):
-                folded = folded + total[at : at + 8]
-            report_ref[lax.div(t, INTERVAL)] = folded
+            total = power(rows - 1, jnp.zeros((width, depth), jnp.float32))
+            at = lax.div(t, INTERVAL)
+            report_ref[pl.ds(at, 1)] += jnp.sum(total, axis=0, keepdims=True)
 
         return carry
 
     lax.fori_loop(0, steps, step, 0)
+
+    def tell(offset):
+        return pltpu.make_async_remote_copy(
+            src_ref=report_ref,
+            dst_ref=got_report.at[me],
+            send_sem=send_report,
+            recv_sem=recv_report,
+            device_id=place(lax.rem(me + offset, everyone)),
+            device_id_type=MESH,
+        )
+
+    def tell_start(offset, carry):
+        tell(offset).start()
+        return carry
+
+    lax.fori_loop(1, everyone, tell_start, 0)
+    got_report[me] = report_ref[...]
     for t in (steps - 2, steps - 1):
         copy_e(t % 2).wait_send()
         copy_w(t % 2).wait_send()
+    everything = got_report.at[pl.ds(0, everyone - 1)]
+    pltpu.make_async_copy(everything, everything, recv_report).wait()
+    pltpu.make_async_copy(everything, everything, send_report).wait()
+
+    def gather(at, held):
+        value = got_report[at]
+        ours = (lax.div(at, slabs) == group).astype(jnp.float32)
+        return held[0] + value, held[1] + ours * value
+
+    zero = jnp.zeros(report_ref.shape, jnp.float32)
+    total, ours = lax.fori_loop(0, everyone, gather, (zero, zero))
+    cells = rows * slabs * width
+    reflected_ref[...] = ours / cells
+    mean_ref[...] = total / cells / groups
 
 
 def one_point(bloch, material, permittivity, peak, sheet, waveform, electric, magnetic):
     rows, width, depth = material.shape
     snaps = waveform.shape[0] // INTERVAL
-    smem = pl.BlockSpec(memory_space=pltpu.SMEM)
+    everyone = lax.axis_size("ka") * lax.axis_size("sp")
+    hbm = pl.BlockSpec(memory_space=pltpu.HBM)
+    lines = -(-snaps // 8) * 8
     vmem = pl.BlockSpec(memory_space=pltpu.VMEM)
     plane = (2, 4, width, depth)
     f32 = jnp.float32
@@ -324,11 +416,22 @@
         out_shape=(
             jax.ShapeDtypeStruct(electric.shape, f32),
             jax.ShapeDtypeStruct(magnetic.shape, f32),
-            jax.ShapeDtypeStruct((snaps, 8, depth), f32),
+            jax.ShapeDtypeStruct((lines, depth), f32),
+            jax.ShapeDtypeStruct((lines, depth), f32),
         ),
-        in_specs=[smem] * 4 + [vmem] * 4,
-        out_specs=(vmem, vmem, vmem),
+        in_specs=[hbm] * 8,
+        out_specs=(vmem, vmem, vmem, vmem),
         scratch_shapes=[
+            pltpu.SMEM(bloch.shape, jnp.int32),
+            pltpu.SMEM(permittivity.shape, f32),
+            pltpu.SMEM(peak.shape, f32),
+            pltpu.SMEM(waveform.shape, f32),
+            pltpu.VMEM(material.shape, jnp.int32),
+            pltpu.VMEM(sheet.shape, f32),
+            pltpu.VMEM(electric.shape, electric.dtype),
+            pltpu.VMEM(magnetic.shape, magnetic.dtype),
+            pltpu.VMEM((lines, depth), f32),
+            pltpu.VMEM((everyone, lines, depth), f32),
             pltpu.VMEM((rows, width, depth), f32),
             pltpu.VMEM((rows, width, depth), f32),
             pltpu.VMEM((2, rows, width, depth), f32),
@@ -340,6 +443,9 @@
             pltpu.SemaphoreType.DMA((2,)),
             pltpu.SemaphoreType.DMA((2,)),
             pltpu.SemaphoreType.DMA((2,)),
+            pltpu.SemaphoreType.DMA((12,)),
+            pltpu.SemaphoreType.DMA,
+            pltpu.SemaphoreType.DMA,
         ],
         compiler_params=pltpu.CompilerParams(
             collective_id=0, has_side_effects=True, vmem_limit_bytes=40 * 1024 * 1024
@@ -358,8 +464,6 @@
     magnetic_in,
 ):
     points = bloch_index.shape[0]
-    rows, width, depth = material.shape
-    slabs = lax.axis_size("sp")
     results = [
         one_point(
             bloch_index[p : p + 1],
@@ -375,10 +479,9 @@
     ]
     electric_out = jnp.concatenate([r[0] for r in results], 0)
     magnetic_out = jnp.concatenate([r[1] for r in results], 0)
-    reports = jnp.stack([jnp.sum(r[2][:, :, PML + 6], axis=1) for r in results], 0)
-    reflected = lax.psum(reports / (rows * slabs * width), "sp")
-    total_points = points * lax.axis_size("ka")
-    reflected_mean = lax.psum(jnp.sum(reflected, 0) / total_points, "ka")
+    snaps = waveform.shape[0] // INTERVAL
+    reflected = jnp.stack([r[2][:snaps, PML + 6] for r in results], 0)
+    reflected_mean = sum(r[3][:snaps, PML + 6] for r in results) / points
     return (electric_out, magnetic_out, reflected, reflected_mean)
 
 

time: 125 us -> 93.8 us (0.75)
  blocking collectives: 36 us -> 0 us
  Pallas kernels: 73.4 us -> 81.6 us
  local copies, waits for them, and re-layouts: 13.8 us -> 10.6 us
    psum x2 -> x0, blocking collectives: 36 us -> none  [the longest x1 31.1 us: on_device(): reflected_mean = lax.psum(jnp.sum(reflected, 0) / total_points, 'ka')]
    pallas_call x1, Pallas kernels: 73.4 us -> 81.6 us  [one_point(): pl.pallas_call(kernel, out_shape=(jax.ShapeDtypeStruct(electric.shape, f3...]
    unnamed x20 -> x16, local copies, waits for them, and re-layouts: 13.8 us -> 9.86 us
where the time goes in v2:
time: 93.8 us; the launch traced here: 93.5 us
  Pallas kernels  81.6 us (87%)
  local copies, waits for them, and re-layouts  10.6 us (11%)
  between operations  1.3 us (1%)
    pallas_call x1, Pallas kernels, one_point(): pl.pallas_call(kernel, out_shape=(jax.ShapeDtypeStruct(electric.shape, f3...  81.6 us
    unnamed x16, local copies, waits for them, and re-layouts  9.86 us

profile of v2, /device:TPU:0, one launch (start us, length us, event | category | flops | bytes accessed | tf_op | source)
XLA Modules:
  0.0 93.5 jit_solution(1742477092649673584)
XLA Ops:
  1.3 0.0 copy-start
  1.3 1.4 %copy-done = bf16[1,6,16,64,128]{4,3,2,1,0:T(8,128)(2,1)S(1)} copy-done((bf16[1,6,16,64,128]{4,3,2,1,0:T(8,128)(2,1)S(1)}, bf16[1,6,16,64,128]{4,3,2,1,0:T(8,128)(2,1)}, u32[]{:S(2)}) %copy-start) | copy-done | bytes 1572888
  2.7 0.0 copy-start.1
  2.7 1.4 %copy-done.1 = bf16[1,6,16,64,128]{4,3,2,1,0:T(8,128)(2,1)S(1)} copy-done((bf16[1,6,16,64,128]{4,3,2,1,0:T(8,128)(2,1)S(1)}, bf16[1,6,16,64,128]{4,3,2,1,0:T(8,128)(2,1)}, u32[]{:S(2)}) %copy-start.1) | copy-done | bytes 1572888
  4.1 0.0 copy-start.2
  4.1 1.0 %copy-done.2 = s32[16,64,128]{2,1,0:T(8,128)S(1)} copy-done((s32[16,64,128]{2,1,0:T(8,128)S(1)}, s32[16,64,128]{2,1,0:T(8,128)}, u32[]{:S(2)}) %copy-start.2) | copy-done | bytes 524312
  5.1 0.0 copy-start.3
  5.1 0.7 copy-done.3
  5.9 0.0 copy-start.4
  5.9 0.7 copy-done.4
  6.5 0.0 copy-start.5
  6.5 0.7 copy-done.5
  7.2 0.0 copy-start.6
  7.2 0.7 copy-done.6
  7.8 81.6 %shard_map.111 = (f32[1,6,16,64,128]{4,3,2,1,0:T(8,128)S(1)}, f32[1,6,16,64,128]{4,3,2,1,0:T(8,128)S(1)}, f32[8,128]{1,0:T(8,128)S(1)}, f32[8,128]{1,0:T(8,128)S(1)}) custom-call(s32[1,2]{1,0:T(1,128)S(1)} %copy-done.4, f32[3]{0:T(128)S(1)} %copy-done.5, f32[1]{0:T(128)S(6)} %copy.14.peak_in, f32[10]{0:T(128)S(1)} %copy-done.6, ...), custom_call_target="tpu_custom_call" | custom-call | tf_op jit(solution)/shard_map/pallas_call | solution.py:414
  89.4 0.7 slice_reduce_fusion
  90.2 1.7 %copy.15 = f32[1,6,16,64,128]{4,3,2,1,0:T(8,128)} copy(f32[1,6,16,64,128]{4,3,2,1,0:T(8,128)S(1)} %get-tuple-element.18) | data formatting | bytes 6291456
  91.8 1.7 %copy.16 = f32[1,6,16,64,128]{4,3,2,1,0:T(8,128)} copy(f32[1,6,16,64,128]{4,3,2,1,0:T(8,128)S(1)} %get-tuple-element.19) | data formatting | bytes 6291456
Async XLA Ops:
  1.3 1.4 %copy-start = (bf16[1,6,16,64,128]{4,3,2,1,0:T(8,128)(2,1)S(1)}, bf16[1,6,16,64,128]{4,3,2,1,0:T(8,128)(2,1)}, u32[]{:S(2)}) copy-start(bf16[1,6,16,64,128]{4,3,2,1,0:T(8,128)(2,1)} %e_hbm.1) | copy-start | bytes 4718596
  2.7 1.4 %copy-start.1 = (bf16[1,6,16,64,128]{4,3,2,1,0:T(8,128)(2,1)S(1)}, bf16[1,6,16,64,128]{4,3,2,1,0:T(8,128)(2,1)}, u32[]{:S(2)}) copy-start(bf16[1,6,16,64,128]{4,3,2,1,0:T(8,128)(2,1)} %h_hbm.1) | copy-start | bytes 4718596
  4.1 1.0 %copy-start.2 = (s32[16,64,128]{2,1,0:T(8,128)S(1)}, s32[16,64,128]{2,1,0:T(8,128)}, u32[]{:S(2)}) copy-start(s32[16,64,128]{2,1,0:T(8,128)} %material_in.1) | copy-start | bytes 1572868
  5.1 0.7 copy-start.3
  5.9 0.7 copy-start.4
  6.5 0.7 copy-start.5
  7.2 0.7 copy-start.6

commit v3 on v2

--- a/solution.py
+++ b/solution.py
@@ -318,48 +318,60 @@
         slot = lax.rem(t, 2)
         later = lax.rem(t + 1, 2)
         drive = wave_ref[t]
-        lax.fori_loop(0, rows - 1, h_plane, 0)
-        hx_plane(rows - 1)
-        copy_w(slot).wait_recv()
-        ey, ez = e_first(slot, drive)
-
-        @pl.when(jnp.logical_and(t >= 1, t < steps - 1))
-        def _():
-            copy_e(later).wait_send()
-
-        @pl.when(t < steps - 1)
-        def _():
-            put_plane(out_e, later, 0, ey)
-            put_plane(out_e, later, 1, ez)
-            copy_e(later).start()
+        even = slot == 0
+        ready = jnp.logical_and(t >= 1, t < steps - 1)
+        snapshot = lax.rem(t + 1, INTERVAL) == 0
+        empty = jnp.zeros((width, depth), jnp.float32)
+
+        def left():
+            copy_w(slot).wait_recv()
+            ey, ez = e_first(slot, drive)
+
+            @pl.when(ready)
+            def _():
+                copy_e(later).wait_send()
+
+            @pl.when(t < steps - 1)
+            def _():
+                put_plane(out_e, later, 0, ey)
+                put_plane(out_e, later, 1, ez)
+                copy_e(later).start()
+
+        def right():
+            copy_e(slot).wait_recv()
+            complete_h(slot)
+            e_update(rows - 1, drive, get(h_ref, 1, rows - 2), get(h_ref, 2, rows - 2))
+
+            @pl.when(ready)
+            def _():
+                copy_w(later).wait_send()
+
+            @pl.when(t < steps - 1)
+            def _():
+                partial_h(later)
+                copy_w(later).start()
 
         def inner(x, held):
             e_update(x, drive, get(h_ref, 1, x - 1), get(h_ref, 2, x - 1))
             return held
 
+        lax.fori_loop(0, rows - 1, h_plane, 0)
+        hx_plane(rows - 1)
+        pl.when(even)(left)
+        pl.when(jnp.logical_not(even))(right)
         lax.fori_loop(1, rows - 1, inner, 0)
 
-        @pl.when(lax.rem(t + 1, INTERVAL) == 0)
+        @pl.when(snapshot)
         def _():
-            total = lax.fori_loop(0, rows - 1, power, jnp.zeros((width, depth), jnp.float32))
+            total = lax.fori_loop(1, rows - 1, power, empty)
             report_ref[pl.ds(lax.div(t, INTERVAL), 1)] = jnp.sum(total, axis=0, keepdims=True)
 
-        copy_e(slot).wait_recv()
-        complete_h(slot)
-        e_update(rows - 1, drive, get(h_ref, 1, rows - 2), get(h_ref, 2, rows - 2))
-
-        @pl.when(jnp.logical_and(t >= 1, t < steps - 1))
+        pl.when(even)(right)
+        pl.when(jnp.logical_not(even))(left)
+
+        @pl.when(snapshot)
         def _():
-            copy_w(later).wait_send()
-
-        @pl.when(t < steps - 1)
-        def _():
-            partial_h(later)
-            copy_w(later).start()
-
-        @pl.when(lax.rem(t + 1, INTERVAL) == 0)
-        def _():
-            total = power(rows - 1, jnp.zeros((width, depth), jnp.float32))
+            total = power(0, power(rows - 1, empty))
             at = lax.div(t, INTERVAL)
             report_ref[pl.ds(at, 1)] += jnp.sum(total, axis=0, keepdims=True)
 

time: 93.8 us -> 82.2 us (0.88)
  Pallas kernels: 81.6 us -> 69.9 us
    pallas_call x1, Pallas kernels: 81.6 us -> 69.9 us  [one_point(): pl.pallas_call(kernel, out_shape=(jax.ShapeDtypeStruct(electric.shape, f3...]
where the time goes in v3:
time: 82.2 us; the launch traced here: 81.8 us
  Pallas kernels  69.9 us (85%)
  local copies, waits for them, and re-layouts  10.6 us (13%)
  between operations  1.3 us (2%)
    pallas_call x1, Pallas kernels, one_point(): pl.pallas_call(kernel, out_shape=(jax.ShapeDtypeStruct(electric.shape, f3...  69.9 us
    unnamed x16, local copies, waits for them, and re-layouts  9.86 us

profile of v3, /device:TPU:0, one launch (start us, length us, event | category | flops | bytes accessed | tf_op | source)
XLA Modules:
  0.0 81.8 jit_solution(9212099769959328441)
XLA Ops:
  1.3 0.0 copy-start
  1.3 1.4 %copy-done = bf16[1,6,16,64,128]{4,3,2,1,0:T(8,128)(2,1)S(1)} copy-done((bf16[1,6,16,64,128]{4,3,2,1,0:T(8,128)(2,1)S(1)}, bf16[1,6,16,64,128]{4,3,2,1,0:T(8,128)(2,1)}, u32[]{:S(2)}) %copy-start) | copy-done | bytes 1572888
  2.7 0.0 copy-start.1
  2.7 1.4 %copy-done.1 = bf16[1,6,16,64,128]{4,3,2,1,0:T(8,128)(2,1)S(1)} copy-done((bf16[1,6,16,64,128]{4,3,2,1,0:T(8,128)(2,1)S(1)}, bf16[1,6,16,64,128]{4,3,2,1,0:T(8,128)(2,1)}, u32[]{:S(2)}) %copy-start.1) | copy-done | bytes 1572888
  4.1 0.0 copy-start.2
  4.1 1.0 %copy-done.2 = s32[16,64,128]{2,1,0:T(8,128)S(1)} copy-done((s32[16,64,128]{2,1,0:T(8,128)S(1)}, s32[16,64,128]{2,1,0:T(8,128)}, u32[]{:S(2)}) %copy-start.2) | copy-done | bytes 524312
  5.1 0.0 copy-start.3
  5.1 0.7 copy-done.3
  5.9 0.0 copy-start.4
  5.9 0.7 copy-done.4
  6.5 0.0 copy-start.5
  6.5 0.7 copy-done.5
  7.2 0.0 copy-start.6
  7.2 0.7 copy-done.6
  7.8 69.9 %shard_map.111 = (f32[1,6,16,64,128]{4,3,2,1,0:T(8,128)S(1)}, f32[1,6,16,64,128]{4,3,2,1,0:T(8,128)S(1)}, f32[8,128]{1,0:T(8,128)S(1)}, f32[8,128]{1,0:T(8,128)S(1)}) custom-call(s32[1,2]{1,0:T(1,128)S(1)} %copy-done.4, f32[3]{0:T(128)S(1)} %copy-done.5, f32[1]{0:T(128)S(6)} %copy.14.peak_in, f32[10]{0:T(128)S(1)} %copy-done.6, ...), custom_call_target="tpu_custom_call" | custom-call | tf_op jit(solution)/shard_map/pallas_call | solution.py:426
  77.8 0.7 slice_reduce_fusion
  78.5 1.7 %copy.15 = f32[1,6,16,64,128]{4,3,2,1,0:T(8,128)} copy(f32[1,6,16,64,128]{4,3,2,1,0:T(8,128)S(1)} %get-tuple-element.18) | data formatting | bytes 6291456
  80.2 1.7 %copy.16 = f32[1,6,16,64,128]{4,3,2,1,0:T(8,128)} copy(f32[1,6,16,64,128]{4,3,2,1,0:T(8,128)S(1)} %get-tuple-element.19) | data formatting | bytes 6291456
Async XLA Ops:
  1.3 1.4 %copy-start = (bf16[1,6,16,64,128]{4,3,2,1,0:T(8,128)(2,1)S(1)}, bf16[1,6,16,64,128]{4,3,2,1,0:T(8,128)(2,1)}, u32[]{:S(2)}) copy-start(bf16[1,6,16,64,128]{4,3,2,1,0:T(8,128)(2,1)} %e_hbm.1) | copy-start | bytes 4718596
  2.7 1.4 %copy-start.1 = (bf16[1,6,16,64,128]{4,3,2,1,0:T(8,128)(2,1)S(1)}, bf16[1,6,16,64,128]{4,3,2,1,0:T(8,128)(2,1)}, u32[]{:S(2)}) copy-start(bf16[1,6,16,64,128]{4,3,2,1,0:T(8,128)(2,1)} %h_hbm.1) | copy-start | bytes 4718596
  4.1 1.0 %copy-start.2 = (s32[16,64,128]{2,1,0:T(8,128)S(1)}, s32[16,64,128]{2,1,0:T(8,128)}, u32[]{:S(2)}) copy-start(s32[16,64,128]{2,1,0:T(8,128)} %material_in.1) | copy-start | bytes 1572868
  5.1 0.7 copy-start.3
  5.9 0.7 copy-start.4
  6.5 0.7 copy-start.5
  7.2 0.7 copy-start.6

commit v4 on v3

--- a/solution.py
+++ b/solution.py
@@ -462,7 +462,7 @@
         compiler_params=pltpu.CompilerParams(
             collective_id=0, has_side_effects=True, vmem_limit_bytes=40 * 1024 * 1024
         ),
-    )(bloch, permittivity, peak, waveform, material, sheet, electric, magnetic)
+    )(*((v if v.shape == (1,) else pltpu.with_memory_space_constraint(v, pltpu.HBM)) for v in (bloch, permittivity, peak, waveform, material, sheet, electric, magnetic)))
 
 
 def on_device(

time: 82.2 us -> 75.1 us (0.914)
  local copies, waits for them, and re-layouts: 10.6 us -> 4.06 us
    unnamed x16 -> x2, local copies, waits for them, and re-layouts: 9.86 us -> 3.33 us
where the time goes in v4:
time: 75.1 us; the launch traced here: 74.9 us
  Pallas kernels  69.6 us (93%)
  local copies, waits for them, and re-layouts  4.06 us (5%)
  between operations  1.29 us (2%)
    pallas_call x1, Pallas kernels, one_point(): pl.pallas_call(kernel, out_shape=(jax.ShapeDtypeStruct(electric.shape, f3...  69.6 us
    unnamed x2, local copies, waits for them, and re-layouts  3.33 us

profile of v4, /device:TPU:0, one launch (start us, length us, event | category | flops | bytes accessed | tf_op | source)
XLA Modules:
  0.0 74.9 jit_solution(548877737845055565)
XLA Ops:
  1.3 69.6 %shard_map.111 = (f32[1,6,16,64,128]{4,3,2,1,0:T(8,128)S(1)}, f32[1,6,16,64,128]{4,3,2,1,0:T(8,128)S(1)}, f32[8,128]{1,0:T(8,128)S(1)}, f32[8,128]{1,0:T(8,128)S(1)}) custom-call(s32[1,2]{1,0:T(1,128)} %bloch_in.1, f32[3]{0:T(128)} %perm_in.1, f32[1]{0:T(128)S(6)} %copy.14.peak_in, f32[10]{0:T(128)} %wave_in.1, s32[16,64,128]{2,1,0:T(8,128)} %material_in.1, ...), custom_call_target="tpu_custom_call" | custom-call | tf_op jit(solution)/shard_map/pallas_call | solution.py:426
  70.9 0.7 slice_reduce_fusion
  71.6 1.7 %copy.15 = f32[1,6,16,64,128]{4,3,2,1,0:T(8,128)} copy(f32[1,6,16,64,128]{4,3,2,1,0:T(8,128)S(1)} %get-tuple-element.18) | data formatting | bytes 6291456
  73.3 1.7 %copy.16 = f32[1,6,16,64,128]{4,3,2,1,0:T(8,128)} copy(f32[1,6,16,64,128]{4,3,2,1,0:T(8,128)S(1)} %get-tuple-element.19) | data formatting | bytes 6291456
